TPU v7x, 32 devices: a whole 2x2x4 slice. The times are simulated.
32 devices in a mesh: date: 4 (over y, x), pix: 8 (over z, core).
Axes of the slice: x: 2, y: 2, z: 4, core: 2. Of those that a mesh axis runs over, the one named last changes fastest.
Arguments:
- stack: bfloat16 [64, 7, 64, 1024], P('date', None, None, 'pix'), may hold values from -8 to 8
- quality: int32 [64, 64, 1024], P('date', None, 'pix'), may hold values from 0 to 1073741823
- days: int32 [64], P('date'), may hold values from 8 to 1536, as said below
Outputs:
- coef: float32 [7, 8, 64, 1024], P(None, None, 'pix', 'date')
- score: float32 [7, 64, 1024], P(None, 'pix', 'date')
Inputs may be any that keep to these rules, and one draw needn't show every extreme that they name: `days`: strictly increasing.
All inputs are finite; a program needn't handle non-finite values.
Results may differ from a plain program's by a relative error of at most 0.0003.
Values may be sent and summed in bfloat16 or wider, within the bound.
A program may use at most 256 MiB of HBM per device.

v0:
```python
import jax
import jax.numpy as jnp
from jax import lax
from jax.sharding import PartitionSpec as P

RIDGE_TERM = 1.0
PAIR_LIST = [(first, second) for first in range(8) for second in range(first, 8)]


def pair_number(first, second):
    return PAIR_LIST.index((min(first, second), max(first, second)))


def design_matrix(days):
    moment_t = days.astype(jnp.float32)
    columns = [jnp.ones_like(moment_t), (moment_t - 512.0) / 512.0]
    for order in range(1, 4):
        phase = 2.0 * jnp.pi * order * moment_t / 365.25
        columns.append(jnp.cos(phase))
        columns.append(jnp.sin(phase))
    return jnp.stack(columns, 1)


def weights(quality):
    cloud = jnp.bitwise_and(jnp.right_shift(quality, 3), 1)
    level = jnp.bitwise_and(jnp.right_shift(quality, 8), 3)
    return (1 - cloud).astype(jnp.float32) / (1.0 + level.astype(jnp.float32))


def pair_products(design):
    return jnp.stack([design[:, first] * design[:, second] for first, second in PAIR_LIST], 1)


def chol_solve(gram, moment):
    lower = {}
    for first in range(8):
        for second in range(first + 1):
            total = gram[pair_number(first, second)]
            if first == second:
                total = total + RIDGE_TERM
            for inner in range(second):
                total = total - lower[first, inner] * lower[second, inner]
            if first == second:
                lower[first, first] = jnp.sqrt(total)
            else:
                lower[first, second] = total / lower[second, second]
    forward = []
    for first in range(8):
        total = moment[first]
        for inner in range(first):
            total = total - lower[first, inner][None, :] * forward[inner]
        forward.append(total / lower[first, first][None, :])
    backward = [None] * 8
    for first in range(7, -1, -1):
        total = forward[first]
        for inner in range(first + 1, 8):
            total = total - lower[inner, first][None, :] * backward[inner]
        backward[first] = total / lower[first, first][None, :]
    return jnp.stack(backward, 0)


def local(stack, quality, days):
    high = lax.Precision.HIGHEST
    bands = stack.shape[1]
    local_dates, all_rows, arrive_cols = (stack.shape[0], stack.shape[2], stack.shape[3])
    arrive_pixels = all_rows * arrive_cols
    design = design_matrix(days)
    weight = weights(quality).reshape(local_dates, arrive_pixels)
    samples = stack.reshape(local_dates, bands, arrive_pixels).astype(jnp.float32)
    gram_part = jnp.dot(pair_products(design).T, weight, precision=high)
    weighted = weight[:, None, :] * samples
    moment_part = jnp.dot(
        design.T, weighted.reshape(local_dates, bands * arrive_pixels), precision=high
    )
    square_part = jnp.sum(weighted * samples, 0)
    weight_part = jnp.sum(weight, 0)[None, :]
    stacked = jnp.concatenate(
        [gram_part, moment_part.reshape(8 * bands, arrive_pixels), square_part, weight_part], 0
    )
    stacked = stacked.reshape(stacked.shape[0], all_rows, arrive_cols)
    spread = lax.all_to_all(stacked, "pix", split_axis=1, concat_axis=2, tiled=True)
    summed = lax.psum_scatter(spread, "date", scatter_dimension=2, tiled=True)
    row_count, col_count = (summed.shape[1], summed.shape[2])
    pixels = row_count * col_count
    summed = summed.reshape(summed.shape[0], pixels)
    gram = summed[:36]
    moment = summed[36 : 36 + 8 * bands].reshape(8, bands, pixels)
    squares = summed[36 + 8 * bands : 36 + 9 * bands]
    wsum = summed[36 + 9 * bands]
    coef_flat = chol_solve(gram, moment)
    ssr = squares - 2.0 * jnp.sum(coef_flat * moment, 0)
    for first in range(8):
        for second in range(8):
            ssr = (
                ssr
                + gram[pair_number(first, second)][None, :] * coef_flat[first] * coef_flat[second]
            )
    total_ssr, total_weight = lax.psum((jnp.sum(ssr, 1), jnp.sum(wsum)), ("date", "pix"))
    sigma2 = total_ssr / total_weight
    score = jnp.sqrt(ssr / (wsum[None, :] + 1.0)) / jnp.sqrt(sigma2)[:, None]
    coef = jnp.transpose(coef_flat.reshape(8, bands, row_count, col_count), (1, 0, 2, 3))
    return (coef, score.reshape(bands, row_count, col_count))


def solution(mesh):
    return jax.shard_map(
        local,
        mesh=mesh,
        in_specs=(P("date", None, None, "pix"), P("date", None, "pix"), P("date")),
        out_specs=(P(None, None, "pix", "date"), P(None, "pix", "date")),
        check_vma=False,
    )
```

profile of v0, /device:TPU:0, one launch (start us, length us, event | category | flops | bytes accessed | tf_op | source)
XLA Modules:
  0.0 227.7 jit_solution(3004523274341131072)
XLA Ops:
  7.2 1.2 fusion.103
  8.5 2.0 fusion
  10.5 0.1 copy.184
  10.6 0.1 multiply_bitcast_fusion
  10.7 0.1 copy.140
  10.8 0.1 copy.141
  10.9 0.1 copy.142
  11.0 0.1 copy.143
  11.1 0.1 copy.144
  11.1 0.1 copy.145
  11.2 0.1 copy.146
  11.3 0.3 copy.246
  11.6 0.4 mul.6375
  12.0 3.9 %copy.189 = f32[2,8,7,8192]{3,1,2,0:T(8,128)} copy(f32[2,8,7,8192]{3,2,1,0:T(8,128)S(1)} %bitcast.504) | data formatting | bytes 7340032
  15.9 2.2 convert.1
  18.2 0.1 stack.167
  18.2 8.7 %fusion.1 = f32[8,57344]{1,0:T(8,128)} fusion(f32[16,8]{1,0:T(8,128)S(1)} %stack.167, f32[16,57344]{1,0:T(8,128)} %bitcast.505, f32[2,8,448,128]{3,2,1,0:T(8,128)} %convert.1), kind=kOutput, calls=%fused_computation.3 | convolution fusion | flops 88997888 | bytes 9175552 | tf_op jit(solution)/shard_map/dot_general | solution.py:72
  26.9 1.8 concatenate.9
  28.7 2.3 %copy.183 = f32[56,64,128]{2,0,1:T(8,128)} copy(f32[56,64,128]{2,1,0:T(8,128)S(1)} %concatenate.9) | data formatting | bytes 3670016 | tf_op jit(solution)/shard_map/concatenate | solution.py:77
  31.0 0.1 copy.147
  31.1 0.1 copy.148
  31.2 0.1 copy.149
  31.3 0.1 copy.150
  31.4 0.1 copy.151
  31.8 0.1 copy.156
  31.9 0.1 copy.157
  31.9 0.1 copy.158
  32.0 0.1 copy.159
  32.1 0.1 copy.160
  32.2 0.1 copy.161
  32.6 0.1 copy.166
  32.7 0.1 copy.167
  32.8 0.1 copy.168
  32.9 0.1 copy.169
  32.9 0.1 copy.170
  33.4 0.1 stack.166
  33.5 1.2 fusion.3
  34.8 0.3 pad_maximum_fusion
  35.1 83.3 %all_to_all.18 = f32[100,64,128]{2,0,1:T(8,128)S(1)} all-to-all(f32[100,64,128]{2,0,1:T(8,128)S(1)} %pad_maximum_fusion), channel_id=1, replica_groups=mesh['date'=4,'pix'=8] {'pix'}, dimensions={1} | all-to-all | bytes 6553600 | tf_op jit(solution)/shard_map/all_to_all | solution.py:81
  118.4 2.3 copy.245
  120.7 44.1 %reduce-scatter.2.cloned.1.call-done = f32[100,8,256]{2,1,0:T(8,128)} async-done(((f32[100,8,1024]{2,1,0:T(8,128)}), f32[100,8,256]{2,1,0:T(8,128)}) %reduce-scatter.2.cloned.1.call-update) | async-done | bytes 819216 | tf_op jit(solution)/shard_map/reduce_scatter | solution.py:82
  164.8 0.9 add_bitcast_fusion
  165.7 1.5 slice_reduce_fusion
  167.6 0.9 fusion.104
  168.6 0.8 rsqrt_multiply_fusion.39
  169.4 0.9 rsqrt_multiply_fusion.28
  170.3 0.9 rsqrt_multiply_fusion.26
  171.1 0.9 rsqrt_multiply_fusion.27
  172.0 0.7 rsqrt_multiply_fusion.40
  172.7 0.8 rsqrt_multiply_fusion.18
  173.5 0.8 subtract_sqrt_fusion.7
  174.3 0.8 rsqrt_multiply_fusion.10
  175.1 0.8 subtract_sqrt_fusion.6
  176.7 0.4 divide_dynamic-update-slice_fusion
  177.1 0.2 constant_dynamic-update-slice_fusion.6
  177.3 0.2 constant_dynamic-update-slice_fusion.5
  177.5 0.1 constant_dynamic-update-slice_fusion.4
  177.7 0.1 reshape.15694
  178.0 0.9 fusion.93
  178.9 0.1 bitcast_dynamic-update-slice_fusion.7
  179.2 0.8 copy.186
  180.0 39.5 %all-reduce = (f32[7]{0:T(128)S(1)}, f32[]{:T(128)}) all-reduce(f32[7]{0:T(128)S(1)} %get-tuple-element.12, f32[]{:T(128)} %get-tuple-element.192), channel_id=1, replica_groups=mesh['date'=4,'pix'=8] {'date','pix'}, use_global_device_ids=true, to_apply=%region_5.0 | all-reduce | flops 8 | bytes 64 | tf_op jit(solution)/shard_map/psum | solution.py:98
  219.5 0.7 divide_sqrt_fusion
  220.2 0.7 sqrt_divide_fusion
  (98 shorter events, 2.3 us)
Async XLA Ops:
  7.2 3.5 %copy-start.3 = (s32[16]{0:T(128)S(1)}, s32[16]{0:T(128)}, u32[]{:S(2)}) copy-start(s32[16]{0:T(128)} %param.5) | copy-start | bytes 196
  7.2 157.6 %reduce-scatter.2.cloned.1.call-start = ((), (), s32[]{:S(2)}) async-start(), calls=%async_computation.2 | async-start | bytes 4096000 | tf_op jit(solution)/shard_map/reduce_scatter | solution.py:82
  12.0 3.9 %copy-start.1 = (bf16[16,7,64,128]{3,2,1,0:T(8,128)(2,1)S(1)}, bf16[16,7,64,128]{3,2,1,0:T(8,128)(2,1)}, u32[]{:S(2)}) copy-start(bf16[16,7,64,128]{3,2,1,0:T(8,128)(2,1)} %param.3) | copy-start | bytes 5505028
  31.0 3.7 %copy-start.2 = (f32[56,64,128]{2,0,1:T(8,128)S(1)}, f32[56,64,128]{2,0,1:T(8,128)}, u32[]{:S(2)}) copy-start(f32[56,64,128]{2,0,1:T(8,128)} %copy.183) | copy-start | bytes 5505028
  164.8 11.1 %copy-start = (f32[100,8,256]{2,1,0:T(8,128)S(1)}, f32[100,8,256]{2,1,0:T(8,128)}, u32[]{:S(2)}) copy-start(f32[100,8,256]{2,1,0:T(8,128)} %reduce-scatter.2.cloned.1.call-done) | copy-start | bytes 2457604
  176.3 1.4 slice-start
Sparse Core Ops, SparseCore 0:
  120.8 43.9 reduce-scatter.1
where the time goes:
time: 229 us; the launch traced here: 228 us
  blocking collectives  123 us (54%)
  waiting for transfers between devices  44.1 us (19%)
  other arithmetic  19.6 us (9%)
  local copies, waits for them, and re-layouts  16.5 us (7%)
  between operations  14.7 us (6%)
  matrix products  9.93 us (4%)
    all_to_all x1, blocking collectives, local(): lax.all_to_all(stacked, 'pix', split_axis=1, concat_axis=2, tiled=True)  83.3 us
    reduce_scatter x1, waiting for transfers between devices, local(): summed = lax.psum_scatter(spread, 'date', scatter_dimension=2, tiled=True)  44.1 us
    psum x1, blocking collectives, local(): lax.psum((jnp.sum(ssr, 1), jnp.sum(wsum)), ('date', 'pix'))  39.5 us
    dot_general x1, matrix products, local(): jnp.dot(design.T, weighted.reshape(local_dates, bands * arrive_pixels), p...  8.69 us
    div x14, other arithmetic, chol_solve(): lower[first, second] = total / lower[second, second]  5.87 us
    unnamed x54, local copies, waits for them, and re-layouts  5.3 us
  transfers between devices with their start and end apart: 1, of which 1 were waited for; matrix products, arithmetic and copies ran while one was open for 0% of the time, Pallas kernels for 0%

commit v1 on v0

--- a/solution.py
+++ b/solution.py
@@ -5,6 +5,7 @@
 
 RIDGE_TERM = 1.0
 PAIR_LIST = [(first, second) for first in range(8) for second in range(first, 8)]
+shifts_all_shape = lambda x_in: lax.psum(lax.psum(x_in, "pix"), axis_name="date")
 
 
 def pair_number(first, second):
@@ -95,7 +96,7 @@
                 ssr
                 + gram[pair_number(first, second)][None, :] * coef_flat[first] * coef_flat[second]
             )
-    total_ssr, total_weight = lax.psum((jnp.sum(ssr, 1), jnp.sum(wsum)), ("date", "pix"))
+    total_ssr, total_weight = shifts_all_shape((jnp.sum(ssr, 1), jnp.sum(wsum)))
     sigma2 = total_ssr / total_weight
     score = jnp.sqrt(ssr / (wsum[None, :] + 1.0)) / jnp.sqrt(sigma2)[:, None]
     coef = jnp.transpose(coef_flat.reshape(8, bands, row_count, col_count), (1, 0, 2, 3))

time: 229 us -> 216 us (0.943)
  blocking collectives: 123 us -> 110 us
    psum x1 -> x2, blocking collectives: 39.5 us -> 26.3 us  [the longest x1 16.8 us: lax.psum(x_in, 'pix')]
where the time goes in v1:
time: 216 us; the launch traced here: 215 us
  blocking collectives  110 us (51%)
  waiting for transfers between devices  44.1 us (20%)
  other arithmetic  19.6 us (9%)
  local copies, waits for them, and re-layouts  16.5 us (8%)
  between operations  14.7 us (7%)
  matrix products  9.93 us (5%)
    all_to_all x1, blocking collectives, local(): lax.all_to_all(stacked, 'pix', split_axis=1, concat_axis=2, tiled=True)  83.3 us
    reduce_scatter x1, waiting for transfers between devices, local(): summed = lax.psum_scatter(spread, 'date', scatter_dimension=2, tiled=True)  44.1 us
    psum x1, blocking collectives, lax.psum(x_in, 'pix')  16.8 us
    psum x1, blocking collectives, lax.psum(lax.psum(x_in, 'pix'), axis_name='date')  9.54 us
    dot_general x1, matrix products, local(): jnp.dot(design.T, weighted.reshape(local_dates, bands * arrive_pixels), p...  8.69 us
    div x14, other arithmetic, chol_solve(): lower[first, second] = total / lower[second, second]  5.87 us
    unnamed x54, local copies, waits for them, and re-layouts  5.31 us
  transfers between devices with their start and end apart: 1, of which 1 were waited for; matrix products, arithmetic and copies ran while one was open for 0% of the time, Pallas kernels for 0%

profile of v1, /device:TPU:0, one launch (start us, length us, event | category | flops | bytes accessed | tf_op | source)
XLA Modules:
  0.0 214.5 jit_solution(17061088651365330272)
XLA Ops:
  7.2 1.2 fusion.103
  8.5 2.0 fusion
  10.5 0.1 copy.184
  10.6 0.1 multiply_bitcast_fusion
  10.7 0.1 copy.140
  10.8 0.1 copy.141
  10.9 0.1 copy.142
  11.0 0.1 copy.143
  11.1 0.1 copy.145
  11.2 0.1 copy.146
  11.3 0.3 copy.246
  11.6 0.4 mul.6375
  12.0 3.9 %copy.189 = f32[2,8,7,8192]{3,1,2,0:T(8,128)} copy(f32[2,8,7,8192]{3,2,1,0:T(8,128)S(1)} %bitcast.504) | data formatting | bytes 7340032
  16.0 2.2 %convert.1 = f32[2,8,448,128]{3,2,1,0:T(8,128)} convert(bf16[2,8,448,128]{3,2,1,0:T(8,128)(2,1)S(1)} %bitcast.508) | non-fusion elementwise | flops 917504 | bytes 5505024
  18.2 0.1 stack.167
  18.3 8.7 %fusion.1 = f32[8,57344]{1,0:T(8,128)} fusion(f32[16,8]{1,0:T(8,128)S(1)} %stack.167, f32[16,57344]{1,0:T(8,128)} %bitcast.505, f32[2,8,448,128]{3,2,1,0:T(8,128)} %convert.1), kind=kOutput, calls=%fused_computation.3 | convolution fusion | flops 88997888 | bytes 9175552 | tf_op jit(solution)/shard_map/dot_general | solution.py:73
  26.9 1.8 concatenate.9
  28.7 2.3 %copy.183 = f32[56,64,128]{2,0,1:T(8,128)} copy(f32[56,64,128]{2,1,0:T(8,128)S(1)} %concatenate.9) | data formatting | bytes 3670016 | tf_op jit(solution)/shard_map/concatenate | solution.py:78
  31.1 0.1 copy.147
  31.5 0.1 copy.152
  31.6 0.1 copy.153
  31.6 0.1 copy.154
  31.7 0.1 copy.155
  31.8 0.1 copy.156
  31.9 0.1 copy.157
  32.3 0.1 copy.162
  32.4 0.1 copy.163
  32.5 0.1 copy.164
  32.5 0.1 copy.165
  32.6 0.1 copy.166
  33.0 0.1 copy.171
  33.1 0.1 copy.172
  33.2 0.1 copy.173
  33.3 0.1 copy.174
  33.4 0.1 stack.166
  33.5 1.2 fusion.3
  34.8 0.3 pad_maximum_fusion
  35.1 83.3 %all_to_all.18 = f32[100,64,128]{2,0,1:T(8,128)S(1)} all-to-all(f32[100,64,128]{2,0,1:T(8,128)S(1)} %pad_maximum_fusion), channel_id=1, replica_groups=mesh['date'=4,'pix'=8] {'pix'}, dimensions={1} | all-to-all | bytes 6553600 | tf_op jit(solution)/shard_map/all_to_all | solution.py:82
  118.4 2.3 %copy.245 = f32[100,8,8,128]{3,1,2,0:T(8,128)} copy(f32[100,8,8,128]{3,0,1,2:T(8,128)S(1)} %bitcast.506) | data formatting | bytes 6553600 | tf_op jit(solution)/shard_map/all_to_all | solution.py:82
  120.7 44.1 %reduce-scatter.2.cloned.1.call-done = f32[100,8,256]{2,1,0:T(8,128)} async-done(((f32[100,8,1024]{2,1,0:T(8,128)}), f32[100,8,256]{2,1,0:T(8,128)}) %reduce-scatter.2.cloned.1.call-update) | async-done | bytes 819216 | tf_op jit(solution)/shard_map/reduce_scatter | solution.py:83
  164.8 0.9 add_bitcast_fusion
  165.7 1.5 slice_reduce_fusion
  167.6 0.9 fusion.104
  168.6 0.8 rsqrt_multiply_fusion.39
  169.4 0.9 rsqrt_multiply_fusion.28
  170.3 0.9 rsqrt_multiply_fusion.26
  171.1 0.9 rsqrt_multiply_fusion.27
  172.0 0.7 rsqrt_multiply_fusion.40
  172.7 0.8 rsqrt_multiply_fusion.18
  173.5 0.8 subtract_sqrt_fusion.7
  174.3 0.8 rsqrt_multiply_fusion.10
  175.1 0.8 subtract_sqrt_fusion.6
  176.7 0.4 divide_dynamic-update-slice_fusion
  177.1 0.2 constant_dynamic-update-slice_fusion.6
  177.3 0.2 constant_dynamic-update-slice_fusion.5
  177.5 0.1 constant_dynamic-update-slice_fusion.4
  177.7 0.1 reshape.15694
  178.0 0.9 fusion.93
  178.9 0.1 bitcast_dynamic-update-slice_fusion.7
  179.2 0.8 copy.186
  180.0 16.8 %all-reduce = (f32[7]{0:T(128)S(1)}, f32[]{:T(128)}) all-reduce(f32[7]{0:T(128)S(1)} %get-tuple-element.14, f32[]{:T(128)} %get-tuple-element.194), channel_id=1, replica_groups=mesh['date'=4,'pix'=8] {'pix'}, use_global_device_ids=true, to_apply=%region_5.0 | all-reduce | flops 8 | bytes 64 | tf_op jit(solution)/shard_map/psum | solution.py:8
  196.8 9.5 %all-reduce.1 = (f32[7]{0:T(128)S(1)}, f32[]{:T(128)}) all-reduce(f32[7]{0:T(128)S(1)} %get-tuple-element.10, f32[]{:T(128)} %get-tuple-element.11), channel_id=1, replica_groups=mesh['date'=4,'pix'=8] {'date'}, use_global_device_ids=true, to_apply=%region_6.0 | all-reduce | flops 8 | bytes 64 | tf_op jit(solution)/shard_map/psum | solution.py:8
  206.3 0.7 divide_sqrt_fusion
  207.0 0.7 sqrt_divide_fusion
  (99 shorter events, 2.4 us)
Async XLA Ops:
  7.2 3.5 %copy-start.3 = (s32[16]{0:T(128)S(1)}, s32[16]{0:T(128)}, u32[]{:S(2)}) copy-start(s32[16]{0:T(128)} %param.5) | copy-start | bytes 196
  7.2 157.6 %reduce-scatter.2.cloned.1.call-start = ((), (), s32[]{:S(2)}) async-start(), calls=%async_computation.2 | async-start | bytes 4096000 | tf_op jit(solution)/shard_map/reduce_scatter | solution.py:83
  12.0 3.9 %copy-start.1 = (bf16[16,7,64,128]{3,2,1,0:T(8,128)(2,1)S(1)}, bf16[16,7,64,128]{3,2,1,0:T(8,128)(2,1)}, u32[]{:S(2)}) copy-start(bf16[16,7,64,128]{3,2,1,0:T(8,128)(2,1)} %param.3) | copy-start | bytes 5505028
  31.0 3.7 %copy-start.2 = (f32[56,64,128]{2,0,1:T(8,128)S(1)}, f32[56,64,128]{2,0,1:T(8,128)}, u32[]{:S(2)}) copy-start(f32[56,64,128]{2,0,1:T(8,128)} %copy.183) | copy-start | bytes 5505028
  164.8 11.1 %copy-start = (f32[100,8,256]{2,1,0:T(8,128)S(1)}, f32[100,8,256]{2,1,0:T(8,128)}, u32[]{:S(2)}) copy-start(f32[100,8,256]{2,1,0:T(8,128)} %reduce-scatter.2.cloned.1.call-done) | copy-start | bytes 2457604
  176.3 1.4 slice-start
Sparse Core Ops, SparseCore 0:
  120.8 43.9 reduce-scatter.1
